TPU v7x, 32 devices: a whole 2x2x4 slice. The times are simulated.
32 devices in a mesh: rep: 2 (over x), zero: 16 (over z, y, core).
Axes of the slice: x: 2, y: 2, z: 4, core: 2. Of those that a mesh axis runs over, the one named last changes fastest.
Arguments:
- acts: bfloat16 [256, 8192], P('rep', 'zero'), may hold values from -6 to 6
- grads_out: bfloat16 [256, 8192], P('rep', 'zero'), may hold values from -12 to 12
- act_inverse: bfloat16 [8192, 8192], P('zero'), as said below
- grad_inverse: bfloat16 [8192, 8192], P('zero'), as said below
Outputs:
- precond: float32 [8192, 8192], P('zero')
Inputs may be any that keep to these rules, and one draw needn't show every extreme that they name: act_inverse is symmetric. grad_inverse is symmetric.
All inputs are finite; a program needn't handle non-finite values.
Results may differ from a plain program's by a relative error of at most 0.004.
Values may be sent and summed in bfloat16 or wider, within the bound.
A program may use at most 128 MiB of HBM per device.

v0:
```python
import jax
import jax.numpy as jnp
from jax import lax
from jax.sharding import PartitionSpec as P


def on_device(acts, grads_out, act_inverse, grad_inverse):
    tok_group = acts.shape[0]
    total_tokens = tok_group * lax.axis_size("rep")
    term = jnp.dot(acts, act_inverse, preferred_element_type=jnp.float32)
    act_pre = lax.psum(term, "zero").astype(jnp.bfloat16)
    grad_pre_t = lax.dot_general(
        grad_inverse,
        lax.all_gather(grads_out, "zero", axis=1, tiled=True),
        (((1,), (1,)), ((), ())),
        preferred_element_type=jnp.float32,
    ).astype(jnp.bfloat16)
    partial_rows = jnp.dot(grad_pre_t, act_pre, preferred_element_type=jnp.float32) / jnp.float32(
        total_tokens
    )
    return lax.psum(partial_rows, "rep")


def solution(mesh):
    return jax.shard_map(
        on_device,
        mesh=mesh,
        in_specs=(P("rep", "zero"), P("rep", "zero"), P("zero", None), P("zero", None)),
        out_specs=P("zero", None),
        check_vma=False,
    )
```

profile of v0, /device:TPU:5, one launch (start us, length us, event | category | flops | bytes accessed | tf_op | source)
XLA Modules:
  0.0 533.4 jit_solution(13765443983158648855)
XLA Ops:
  6.5 0.0 copy-start
  6.5 0.0 all-gather.2.cloned.1.call-start
  6.5 0.7 all-gather.2.cloned.1.call-update
  7.3 0.0 all-reduce.3.cloned.1.call-start
  7.3 0.1 copy-done
  7.4 6.7 %fusion.1 = f32[128,8192]{1,0:T(8,128)} fusion(bf16[128,512]{1,0:T(8,128)(2,1)S(1)} %copy-done, bf16[512,8192]{1,0:T(8,128)(2,1)} %param.6), kind=kOutput, calls=%fused_computation.3 | convolution fusion | flops 1073741824 | bytes 12713984 | tf_op jit(solution)/shard_map/dot_general | solution.py:10
  14.1 103.4 %all-reduce.4 = bf16[128,8192]{1,0:T(8,128)(2,1)S(1)} all-reduce(f32[128,8192]{1,0:T(8,128)} %fusion.1), channel_id=1, replica_groups=mesh['rep'=2,'zero'=16] {'zero'}, use_global_device_ids=true, to_apply=%region_0.0 | all-reduce | flops 1048576 | bytes 6291456 | tf_op jit(solution)/shard_map/psum | solution.py:11
  117.5 0.0 all-gather.2.cloned.1.call-done
  117.5 19.0 %convolution_multiply_fusion = f32[512,8192]{1,0:T(8,128)} fusion(bf16[128,8192]{1,0:T(8,128)(2,1)S(1)} %all-reduce.4, bf16[512,8192]{1,0:T(8,128)(2,1)} %param.7, bf16[128,8192]{1,0:T(8,128)(2,1)} %all-gather.2.cloned.1.call-done), kind=kOutput, calls=%fused_computation | convolution fusion | flops 2151743488 | bytes 29360128 | tf_op jit(solution)/shard_map/dot_general | solution.py:18
  136.4 0.0 all-reduce.3.cloned.1.call-update
  136.5 378.4 %all-reduce.3.cloned.1.call-done = f32[512,8192]{1,0:T(8,128)} async-done(((f32[512,8192]{1,0:T(8,128)}), f32[512,8192]{1,0:T(8,128)}) %all-reduce.3.cloned.1.call-update) | async-done | bytes 16777232 | tf_op jit(solution)/shard_map/psum | solution.py:21
  514.9 0.0 copy-start.1
  514.9 11.7 %copy.8 = f32[512,8192]{1,0:T(8,128)} copy(f32[512,8192]{1,0:T(8,128)} %all-reduce.3.cloned.1.call-done) | data formatting | bytes 33554432
  526.6 0.0 copy-done.1
Async XLA Ops:
  6.5 0.9 copy-start
  6.5 110.9 %all-gather.2.cloned.1.call-start = ((), (), s32[]{:S(2)}) async-start(), calls=%async_computation | async-start | bytes 2228224 | tf_op jit(solution)/shard_map/all_gather | solution.py:14
  7.3 507.7 %all-reduce.3.cloned.1.call-start = ((), (), s32[]{:S(2)}) async-start(), calls=%async_computation.1 | async-start | bytes 33554432 | tf_op jit(solution)/shard_map/psum | solution.py:21
  514.9 11.7 %copy-start.1 = (bf16[128,512]{1,0:T(8,128)(2,1)S(1)}, bf16[128,512]{1,0:T(8,128)(2,1)}, u32[]{:S(2)}) copy-start(bf16[128,512]{1,0:T(8,128)(2,1)} %param.4) | copy-start | bytes 393220
Sparse Core Ops, SparseCore 0:
  9.5 55.2 all-gather.1
  136.6 378.2 all-reduce.2
where the time goes:
time: 535 us; the launch traced here: 533 us
  waiting for transfers between devices  379 us (71%)
  blocking collectives  103 us (19%)
  matrix products  25.6 us (5%)
  between operations  13.4 us (3%)
  local copies, waits for them, and re-layouts  11.8 us (2%)
    psum x1, waiting for transfers between devices, on_device(): return lax.psum(partial_rows, 'rep')  378 us
    psum x1, blocking collectives, on_device(): act_pre = lax.psum(term, 'zero').astype(jnp.bfloat16)  103 us
    dot_general x1, matrix products, on_device(): jnp.dot(grad_pre_t, act_pre, preferred_element_type=jnp.float32)  19 us
    unnamed x5, local copies, waits for them, and re-layouts  11.8 us
  transfers between devices with their start and end apart: 2, of which 1 were waited for; matrix products, arithmetic and copies ran while one was open for 1% of the time, Pallas kernels for 0%

commit v1 on v0

v1 whole, which is shorter than its diff:
```python
import jax
import jax.numpy as jnp
from jax import lax
from jax.sharding import PartitionSpec as P

NT = (((1,), (1,)), ((), ()))


def on_device(acts, grads_out, act_inverse, grad_inverse):
    group = acts.shape[0]
    total_tokens = group * lax.axis_size("rep")
    both = lax.all_gather(jnp.concatenate([acts, grads_out], 0), "zero", axis=1, tiled=True)
    act_own = lax.dot_general(
        both[:group], act_inverse, NT, preferred_element_type=jnp.float32
    ).astype(jnp.bfloat16)
    act_pre = lax.all_gather(act_own, ("rep", "zero"), axis=0)
    grad_own = lax.dot_general(
        both[group:], grad_inverse, NT, preferred_element_type=jnp.float32
    ).astype(jnp.bfloat16)
    grad_pre = lax.all_gather(grad_own, "rep", axis=0, tiled=True)
    zero = lax.axis_size("zero")
    act_pre = act_pre.reshape(-1, zero, group, act_own.shape[1]).transpose(0, 2, 1, 3)
    act_pre = act_pre.reshape(total_tokens, -1)
    summed = lax.dot_general(
        grad_pre, act_pre, (((0,), (0,)), ((), ())), preferred_element_type=jnp.float32
    )
    return summed / jnp.float32(total_tokens)


def solution(mesh):
    return jax.shard_map(
        on_device,
        mesh=mesh,
        in_specs=(P("rep", "zero"), P("rep", "zero"), P("zero", None), P("zero", None)),
        out_specs=P("zero", None),
        check_vma=False,
    )
```

time: 535 us -> 157 us (0.29)
  waiting for transfers between devices: 379 us -> 103 us
  blocking collectives: 103 us -> 5.83 us
    psum x1 -> x0, waiting for transfers between devices: 378 us -> none  [on_device(): return lax.psum(partial_rows, 'rep')]
    psum x1 -> x0, blocking collectives: 103 us -> none  [on_device(): act_pre = lax.psum(term, 'zero').astype(jnp.bfloat16)]
    all_gather x1 -> x2, waiting for transfers between devices: 0.02 us -> 103 us  [the longest x1 55.3 us: on_device(): lax.all_gather(jnp.concatenate([acts, grads_out], 0), 'zero', axis=1, til...]
    unnamed x5 -> x1, local copies, waits for them, and re-layouts: 11.8 us -> 4.3 us
    all_gather x0 -> x1, blocking collectives: none -> 5.83 us  [on_device(): grad_pre = lax.all_gather(grad_own, 'rep', axis=0, tiled=True)]
    dot_general x2 -> x3, matrix products: 25.6 us -> 23.1 us  [the longest x1 8.53 us: on_device(): lax.dot_general(grad_pre, act_pre, (((0,), (0,)), ((), ())), preferred_el...]
  transfers between devices with their start and end apart: 2 -> 2, of which waited for: 1 -> 2; matrix products, arithmetic and copies ran while one was open for 1% -> 4% of each run, Pallas kernels for 0% -> 0%
where the time goes in v1:
time: 157 us; the launch traced here: 156 us
  waiting for transfers between devices  103 us (66%)
  matrix products  23.1 us (15%)
  between operations  13.4 us (9%)
  local copies, waits for them, and re-layouts  8.83 us (6%)
  blocking collectives  5.83 us (4%)
  other arithmetic  1.69 us (1%)
    all_gather x1, waiting for transfers between devices, on_device(): lax.all_gather(jnp.concatenate([acts, grads_out], 0), 'zero', axis=1, til...  55.3 us
    all_gather x1, waiting for transfers between devices, on_device(): act_pre = lax.all_gather(act_own, ('rep', 'zero'), axis=0)  47.9 us
    dot_general x1, matrix products, on_device(): lax.dot_general(grad_pre, act_pre, (((0,), (0,)), ((), ())), preferred_el...  8.53 us
    dot_general x1, matrix products, on_device(): lax.dot_general(both[:group], act_inverse, NT, preferred_element_type=jnp...  7.6 us
    dot_general x1, matrix products, on_device(): lax.dot_general(both[group:], grad_inverse, NT, preferred_element_type=jn...  6.95 us
    all_gather x1, blocking collectives, on_device(): grad_pre = lax.all_gather(grad_own, 'rep', axis=0, tiled=True)  5.83 us
    reshape x1, local copies, waits for them, and re-layouts, on_device(): act_pre.reshape(-1, zero, group, act_own.shape[1]).transpose(0, 2, 1, 3)  4.53 us
    unnamed x1, local copies, waits for them, and re-layouts  4.3 us
  transfers between devices with their start and end apart: 2, of which 2 were waited for; matrix products, arithmetic and copies ran while one was open for 4% of the time, Pallas kernels for 0%

profile of v1, /device:TPU:5, one launch (start us, length us, event | category | flops | bytes accessed | tf_op | source)
XLA Modules:
  0.0 156.1 jit_solution(17112583432541614135)
XLA Ops:
  6.5 0.0 all-gather.4.cloned.1.call-start
  6.5 1.7 %pad_maximum_fusion = bf16[256,512]{1,0:T(8,128)(2,1)} fusion(bf16[128,512]{1,0:T(8,128)(2,1)} %param.5, bf16[128,512]{1,0:T(8,128)(2,1)} %param.4), kind=kLoop, calls=%fused_computation.7 | loop fusion | flops 524288 | bytes 524288 | tf_op jit(solution)/shard_map/concatenate | solution.py:12
  8.2 0.0 all-gather.4.cloned.1.call-update
  8.2 0.0 all-gather.6.cloned.1.call-start
  8.3 55.3 %all-gather.4.cloned.1.call-done = bf16[256,8192]{1,0:T(8,128)(2,1)} async-done(((bf16[256,512]{1,0:T(8,128)(2,1)}), bf16[256,8192]{1,0:T(8,128)(2,1)}) %all-gather.4.cloned.1.call-update) | async-done | bytes 4194320 | tf_op jit(solution)/shard_map/all_gather | solution.py:12
  63.6 7.6 %fusion.7 = bf16[128,512]{1,0:T(8,128)(2,1)} fusion(bf16[512,8192]{1,0:T(8,128)(2,1)} %param.6, bf16[256,8192]{1,0:T(8,128)(2,1)} %all-gather.4.cloned.1.call-done), kind=kOutput, calls=%fused_computation.6 | convolution fusion | flops 1073807360 | bytes 10616832 | tf_op jit(solution)/shard_map/dot_general | solution.py:13
  71.2 0.0 all-gather.6.cloned.1.call-update
  71.2 6.9 %fusion.4 = bf16[128,512]{1,0:T(8,128)(2,1)S(1)} fusion(bf16[512,8192]{1,0:T(8,128)(2,1)} %param.7, bf16[256,8192]{1,0:T(8,128)(2,1)} %all-gather.4.cloned.1.call-done), kind=kOutput, calls=%fused_computation.5 | convolution fusion | flops 1073807360 | bytes 10616832 | tf_op jit(solution)/shard_map/dot_general | solution.py:17
  78.2 5.8 %all_gather.13 = bf16[256,512]{1,0:T(8,128)(2,1)S(1)} all-gather(bf16[128,512]{1,0:T(8,128)(2,1)S(1)} %fusion.4), channel_id=1, replica_groups=mesh['rep'=2,'zero'=16] {'rep'}, dimensions={0}, use_global_device_ids=true | all-gather | bytes 393216 | tf_op jit(solution)/shard_map/all_gather | solution.py:20
  84.0 47.9 %all-gather.6.cloned.1.call-done = bf16[4096,512]{1,0:T(8,128)(2,1)} async-done(((bf16[128,512]{1,0:T(8,128)(2,1)}), bf16[4096,512]{1,0:T(8,128)(2,1)}) %all-gather.6.cloned.1.call-update) | async-done | bytes 4194320 | tf_op jit(solution)/shard_map/all_gather | solution.py:16
  131.8 4.5 %copy.5 = bf16[2,16,128,512]{3,1,2,0:T(8,128)(2,1)S(1)} copy(bf16[2,16,128,512]{3,2,1,0:T(8,128)(2,1)} %bitcast.11) | data formatting | bytes 8388608 | tf_op jit(solution)/shard_map/reshape | solution.py:22
  136.4 4.3 %copy.6 = bf16[32,8,16,512]{3,1,2,0:T(8,128)(2,1)S(1)} copy(bf16[32,8,16,512]{3,2,1,0:T(8,128)(2,1)S(1)} %bitcast.9) | data formatting | bytes 8388608
  140.7 8.5 %convolution_multiply_fusion = f32[512,8192]{1,0:T(8,128)} fusion(bf16[256,512]{1,0:T(8,128)(2,1)S(1)} %all_gather.13, bf16[256,8192]{1,0:T(8,128)(2,1)S(1)} %bitcast.10), kind=kOutput, calls=%fused_computation | convolution fusion | flops 2151677952 | bytes 21233664 | tf_op jit(solution)/shard_map/dot_general | solution.py:24
Async XLA Ops:
  6.5 57.1 %all-gather.4.cloned.1.call-start = ((), (), s32[]{:S(2)}) async-start(), calls=%async_computation | async-start | bytes 4456448 | tf_op jit(solution)/shard_map/all_gather | solution.py:12
  8.2 123.6 %all-gather.6.cloned.1.call-start = ((), (), s32[]{:S(2)}) async-start(), calls=%async_computation.1 | async-start | bytes 4325376 | tf_op jit(solution)/shard_map/all_gather | solution.py:16
Sparse Core Ops, SparseCore 0:
  9.5 54.0 all-gather.3
  71.3 60.4 all-gather.5

commit v2 on v1

--- a/solution.py
+++ b/solution.py
@@ -1,12 +1,16 @@
+import functools
+
 import jax
 import jax.numpy as jnp
 from jax import lax
+from jax.experimental import pallas as pl
+from jax.experimental.pallas import tpu as pltpu
 from jax.sharding import PartitionSpec as P
 
 NT = (((1,), (1,)), ((), ()))
 
 
-def on_device(acts, grads_out, act_inverse, grad_inverse):
+def gathered(acts, grads_out, act_inverse, grad_inverse):
     group = acts.shape[0]
     total_tokens = group * lax.axis_size("rep")
     both = lax.all_gather(jnp.concatenate([acts, grads_out], 0), "zero", axis=1, tiled=True)
@@ -27,6 +31,260 @@
     return summed / jnp.float32(total_tokens)
 
 
+MESH = pl.DeviceIdType.MESH
+
+
+def gather_kernel(
+    outer, acts, grads, a_hbm, g_hbm, act_out, grad_out,
+    a_rows, g_rows, held, pre, grad_pre, acc_a, acc_g,
+    w_sem, send1, recv1, send2, recv2, x_send, x_recv, out_sem,
+):
+    width = acts.shape[1]
+    zero = outer * 4
+    rep = lax.axis_index("rep")
+    me = lax.axis_index("zero")
+    z, y, c = me // 4, (me // 2) % 2, me % 2
+    other_y, other_c, other_rep = 1 - y, 1 - c, 1 - rep
+
+    def at(dz, yy, cc):
+        return ((z + dz) % outer) * 4 + yy * 2 + cc
+
+    loads = [
+        pltpu.make_async_copy(a_hbm, a_rows, w_sem.at[0]),
+        pltpu.make_async_copy(g_hbm, g_rows, w_sem.at[1]),
+    ]
+    for load in loads:
+        load.start()
+
+    hops = list(range(1, outer))
+    hops.sort(key=lambda d: min(d, outer - d))
+    peers = [(rep, at(d, y, c)) for d in hops]
+    peers += [(rep, at(0, other_y, c)), (rep, at(0, y, other_c)), (other_rep, me)]
+    barrier = pltpu.get_barrier_semaphore()
+    for peer in peers:
+        pl.semaphore_signal(barrier, inc=1, device_id=peer, device_id_type=MESH)
+    pl.semaphore_wait(barrier, len(peers))
+
+    own = (acts, grads)
+    sent = []
+
+    def send1_to(q, slot, block, source, peer):
+        copy = pltpu.make_async_remote_copy(
+            src_ref=source, dst_ref=held.at[q, block],
+            send_sem=send1.at[q, slot], recv_sem=recv1.at[q, block],
+            device_id=peer, device_id_type=MESH,
+        )
+        copy.start()
+        sent.append(copy)
+
+    def wait1(q, block):
+        pltpu.make_async_copy(held.at[q, block], held.at[q, block], recv1.at[q, block]).wait()
+
+    z_peer = {d: (rep, at(d, y, c)) for d in hops}
+    y_peer = (rep, at(0, other_y, c))
+    c_peer = (rep, at(0, y, other_c))
+    y_slot, c_slot = outer, 2 * outer
+
+    for q in range(2):
+        for d in hops:
+            send1_to(q, d, me, own[q], z_peer[d])
+        send1_to(q, y_slot, me, own[q], y_peer)
+        send1_to(q, c_slot, me, own[q], c_peer)
+
+    def columns(block):
+        return pl.ds(pl.multiple_of(block * width, width), width)
+
+    def add(q, block, value):
+        if q == 0:
+            acc_a[...] += lax.dot_general(
+                value, a_rows[:, columns(block)], NT, preferred_element_type=jnp.float32
+            )
+        else:
+            acc_g[...] += lax.dot_general(
+                g_rows[:, columns(block)], value, NT, preferred_element_type=jnp.float32
+            )
+
+    def from_z(q, ds):
+        for d in ds:
+            block = at(d, y, c)
+            wait1(q, block)
+            send1_to(q, y_slot + d, block, held.at[q, block], y_peer)
+            send1_to(q, c_slot + d, block, held.at[q, block], c_peer)
+
+    def from_y(q):
+        for d in [0] + hops:
+            block = at(d, other_y, c)
+            wait1(q, block)
+            send1_to(q, c_slot + outer + d, block, held.at[q, block], c_peer)
+
+    def add_mine(q):
+        @pl.loop(0, outer * 2)
+        def _(k):
+            block = (k // 2) * 4 + (k % 2) * 2 + c
+
+            @pl.when(block != me)
+            def _():
+                add(q, block, held[q, block])
+
+    def add_partner(q):
+        for yy in (y, other_y):
+            for d in [0] + hops:
+                wait1(q, at(d, yy, other_c))
+
+        @pl.loop(0, outer * 2)
+        def _(k):
+            block = (k // 2) * 4 + (k % 2) * 2 + other_c
+            add(q, block, held[q, block])
+
+    acc_a[...] = jnp.zeros_like(acc_a)
+    acc_g[...] = jnp.zeros_like(acc_g)
+    loads[0].wait()
+    add(0, me, acts[...])
+    from_z(0, hops)
+    from_y(0)
+    from_z(1, hops[:-1])
+    add_mine(0)
+    add_partner(0)
+
+    rep1, y1 = (rep + c) % 2, (y + 1 - c) % 2
+    rep2, y2 = (rep + 1 - c) % 2, (y + c) % 2
+    rep3, y3 = (rep2 + c) % 2, (y2 + 1 - c) % 2
+
+    def send2_to(slot, block, peer):
+        copy = pltpu.make_async_remote_copy(
+            src_ref=pre.at[block], dst_ref=pre.at[block],
+            send_sem=send2.at[slot], recv_sem=recv2.at[block],
+            device_id=peer, device_id_type=MESH,
+        )
+        copy.start()
+        sent.append(copy)
+
+    def wait2(block):
+        pltpu.make_async_copy(pre.at[block], pre.at[block], recv2.at[block]).wait()
+
+    first_peer = (rep1, at(0, y1, c))
+    second_peer = (rep2, at(0, y2, c))
+    s1, s2, s3 = outer, 2 * outer, 4 * outer
+    mine = rep * zero + me
+    pre[mine] = acc_a[...].astype(jnp.bfloat16)
+
+    from_z(1, hops[-1:])
+    for d in hops:
+        send2_to(d, mine, z_peer[d])
+    send2_to(s1, mine, first_peer)
+    send2_to(s2, mine, second_peer)
+    send2_to(s3, mine, c_peer)
+
+    loads[1].wait()
+    add(1, me, grads[...])
+    from_y(1)
+    for d in hops:
+        block = rep * zero + at(d, y, c)
+        wait2(block)
+        send2_to(s1 + d, block, first_peer)
+        send2_to(s2 + d, block, second_peer)
+        send2_to(s3 + d, block, c_peer)
+    add_mine(1)
+    add_partner(1)
+    grad_pre[rep] = acc_g[...].astype(jnp.bfloat16)
+    for i, d in enumerate([0] + hops):
+        block = rep1 * zero + at(d, y1, c)
+        wait2(block)
+        send2_to(s2 + outer + d, block, second_peer)
+        send2_to(s3 + outer + d, block, c_peer)
+        if i == 0:
+            swap = pltpu.make_async_remote_copy(
+                src_ref=grad_pre.at[rep], dst_ref=grad_pre.at[rep],
+                send_sem=x_send, recv_sem=x_recv,
+                device_id=(other_rep, me), device_id_type=MESH,
+            )
+            swap.start()
+    for part, (rr, yy) in enumerate(((rep2, y2), (rep3, y3))):
+        for d in [0] + hops:
+            block = rr * zero + at(d, yy, c)
+            wait2(block)
+            send2_to(s3 + (2 + part) * outer + d, block, c_peer)
+    swap.wait()
+    grad_done = pltpu.make_async_copy(grad_pre, grad_out, out_sem.at[0])
+    grad_done.start()
+    for rr in (rep, other_rep):
+        for yy in (y, other_y):
+            for d in [0] + hops:
+                wait2(rr * zero + at(d, yy, other_c))
+    act_done = pltpu.make_async_copy(pre, act_out, out_sem.at[1])
+    act_done.start()
+    for copy in sent:
+        copy.wait_send()
+    grad_done.wait()
+    act_done.wait()
+
+
+def product_kernel(tokens, grad_ref, act_ref, out_ref):
+    reps, _, group, width = act_ref.shape
+    rows = jnp.concatenate([grad_ref[r] for r in range(reps)], axis=1)
+    summed = jnp.dot(
+        rows, act_ref[...].reshape(reps * group, width), preferred_element_type=jnp.float32
+    )
+    out_ref[...] = summed / jnp.float32(tokens)
+
+
+def fused(acts, grads_out, act_inverse, grad_inverse):
+    group, width = acts.shape
+    zero = lax.axis_size("zero")
+    reps = lax.axis_size("rep")
+    rows, cols = act_inverse.shape
+    outer = zero // 4
+    bf16, dma = jnp.bfloat16, pltpu.SemaphoreType.DMA
+    vmem = pl.BlockSpec(memory_space=pltpu.VMEM)
+    hbm = pl.BlockSpec(memory_space=pl.ANY)
+    act_pre, grad_pre = pl.pallas_call(
+        functools.partial(gather_kernel, outer),
+        out_shape=(
+            jax.ShapeDtypeStruct((reps * zero, group, width), bf16),
+            jax.ShapeDtypeStruct((reps, width, group), bf16),
+        ),
+        in_specs=[vmem, vmem, hbm, hbm],
+        out_specs=(hbm, hbm),
+        scratch_shapes=[
+            pltpu.VMEM((rows, cols), bf16),
+            pltpu.VMEM((rows, cols), bf16),
+            pltpu.VMEM((2, zero, group, width), bf16),
+            pltpu.VMEM((reps * zero, group, width), bf16),
+            pltpu.VMEM((reps, width, group), bf16),
+            pltpu.VMEM((group, width), jnp.float32),
+            pltpu.VMEM((width, group), jnp.float32),
+            dma((2,)),
+            dma((2, 4 * outer)),
+            dma((2, zero)),
+            dma((8 * outer,)),
+            dma((reps * zero,)),
+            dma,
+            dma,
+            dma((2,)),
+        ],
+        compiler_params=pltpu.CompilerParams(
+            collective_id=0, has_side_effects=True, vmem_limit_bytes=48 * 1024 * 1024
+        ),
+    )(acts, grads_out, act_inverse, grad_inverse)
+    return pl.pallas_call(
+        functools.partial(product_kernel, reps * group),
+        grid=(zero,),
+        out_shape=jax.ShapeDtypeStruct((rows, cols), jnp.float32),
+        in_specs=[
+            pl.BlockSpec((reps, width, group), lambda i: (0, 0, 0)),
+            pl.BlockSpec((reps, 1, group, width), lambda i: (0, i, 0, 0)),
+        ],
+        out_specs=pl.BlockSpec((rows, width), lambda i: (0, i)),
+    )(grad_pre, act_pre.reshape(reps, zero, group, width))
+
+
+def on_device(acts, grads_out, act_inverse, grad_inverse):
+    whole = acts.shape[1] % 128 == 0 and acts.shape[0] % 128 == 0
+    if whole and lax.axis_size("rep") == 2 and lax.axis_size("zero") % 4 == 0 and lax.axis_size("zero") > 4:
+        return fused(acts, grads_out, act_inverse, grad_inverse)
+    return gathered(acts, grads_out, act_inverse, grad_inverse)
+
+
 def solution(mesh):
     return jax.shard_map(
         on_device,

time: 157 us -> 78.5 us (0.50)
  waiting for transfers between devices: 103 us -> 0 us
  Pallas kernels: 0 us -> 73.6 us
  matrix products: 23.1 us -> 0 us
  between operations: 13.4 us -> 0.02 us
  blocking collectives: 5.83 us -> 0 us
  local copies, waits for them, and re-layouts: 8.83 us -> 4.44 us
  other arithmetic: 1.69 us -> 0 us
    all_gather x2 -> x0, waiting for transfers between devices: 103 us -> none  [the longest x1 55.3 us: on_device(): lax.all_gather(jnp.concatenate([acts, grads_out], 0), 'zero', axis=1, til...]
    pallas_call x0 -> x2, Pallas kernels: none -> 73.6 us  [the longest x1 59.4 us: fused(): pl.pallas_call(functools.partial(gather_kernel, outer), out_shape=(jax.Sh...]
    dot_general x3 -> x0, matrix products: 23.1 us -> none  [the longest x1 8.53 us: on_device(): lax.dot_general(grad_pre, act_pre, (((0,), (0,)), ((), ())), preferred_el...]
    all_gather x1 -> x0, blocking collectives: 5.83 us -> none  [on_device(): grad_pre = lax.all_gather(grad_own, 'rep', axis=0, tiled=True)]
    reshape x1 -> x0, local copies, waits for them, and re-layouts: 4.53 us -> none  [on_device(): act_pre.reshape(-1, zero, group, act_own.shape[1]).transpose(0, 2, 1, 3)]
    concatenate x1 -> x0, other arithmetic: 1.69 us -> none  [on_device(): jnp.concatenate([acts, grads_out], 0)]
    unnamed x1 -> x8, local copies, waits for them, and re-layouts: 4.3 us -> 4.44 us
  transfers between devices with their start and end apart: 2 -> 0, of which waited for: 2 -> 0; matrix products, arithmetic and copies ran while one was open for 4% -> 0% of each run, Pallas kernels for 0% -> 0%
where the time goes in v2:
time: 78.5 us; the launch traced here: 78 us
  Pallas kernels  73.6 us (94%)
  local copies, waits for them, and re-layouts  4.44 us (6%)
    pallas_call x1, Pallas kernels, fused(): pl.pallas_call(functools.partial(gather_kernel, outer), out_shape=(jax.Sh...  59.4 us
    pallas_call x1, Pallas kernels, fused(): pl.pallas_call(functools.partial(product_kernel, reps * group), grid=(zer...  14.1 us
    unnamed x8, local copies, waits for them, and re-layouts  4.44 us

profile of v2, /device:TPU:5, one launch (start us, length us, event | category | flops | bytes accessed | tf_op | source)
XLA Modules:
  0.0 78.0 jit_solution(9811159713600253692)
XLA Ops:
  0.0 0.0 copy-start.2
  0.0 0.9 %copy-done.2 = bf16[128,512]{1,0:T(8,128)(2,1)S(1)} copy-done((bf16[128,512]{1,0:T(8,128)(2,1)S(1)}, bf16[128,512]{1,0:T(8,128)(2,1)}, u32[]{:S(2)}) %copy-start.2) | copy-done | bytes 131096
  0.9 0.0 copy-start.3
  0.9 0.9 %copy-done.3 = bf16[128,512]{1,0:T(8,128)(2,1)S(1)} copy-done((bf16[128,512]{1,0:T(8,128)(2,1)S(1)}, bf16[128,512]{1,0:T(8,128)(2,1)}, u32[]{:S(2)}) %copy-start.3) | copy-done | bytes 131096
  1.8 59.4 %shard_map.46 = (bf16[32,128,512]{2,1,0:T(8,128)(2,1)S(1)}, bf16[2,512,128]{2,1,0:T(8,128)(2,1)S(1)}) custom-call(bf16[128,512]{1,0:T(8,128)(2,1)S(1)} %copy-done.2, bf16[128,512]{1,0:T(8,128)(2,1)S(1)} %copy-done.3, bf16[512,8192]{1,0:T(8,128)(2,1)} %a_hbm.1, bf16[512,8192]{1,0:T(8,128)(2,1)} %g_hbm.1), custom_call_target="tpu_custom_call" | custom-call | tf_op jit(solution)/shard_map/pallas_call | solution.py:240
  61.2 0.0 copy-start
  61.3 1.9 %copy-done = bf16[32,128,512]{2,1,0:T(8,128)(2,1)} copy-done((bf16[32,128,512]{2,1,0:T(8,128)(2,1)}, bf16[32,128,512]{2,1,0:T(8,128)(2,1)S(1)}, u32[]{:S(2)}) %copy-start) | copy-done | bytes 4194328
  63.2 0.0 copy-start.1
  63.2 0.7 copy-done.1
  63.9 14.1 %shard_map.47 = f32[512,8192]{1,0:T(8,128)} custom-call(bf16[2,512,128]{2,1,0:T(8,128)(2,1)} %copy-done.1, bf16[2,16,128,512]{3,2,1,0:T(8,128)(2,1)} %bitcast.1), custom_call_target="tpu_custom_call" | custom-call | tf_op jit(solution)/shard_map/pallas_call | solution.py:269
Async XLA Ops:
  0.0 0.9 %copy-start.2 = (bf16[128,512]{1,0:T(8,128)(2,1)S(1)}, bf16[128,512]{1,0:T(8,128)(2,1)}, u32[]{:S(2)}) copy-start(bf16[128,512]{1,0:T(8,128)(2,1)} %acts.1) | copy-start | bytes 393220
  0.9 0.9 %copy-start.3 = (bf16[128,512]{1,0:T(8,128)(2,1)S(1)}, bf16[128,512]{1,0:T(8,128)(2,1)}, u32[]{:S(2)}) copy-start(bf16[128,512]{1,0:T(8,128)(2,1)} %grads.1) | copy-start | bytes 393220
  61.2 1.9 %copy-start = (bf16[32,128,512]{2,1,0:T(8,128)(2,1)}, bf16[32,128,512]{2,1,0:T(8,128)(2,1)S(1)}, u32[]{:S(2)}) copy-start(bf16[32,128,512]{2,1,0:T(8,128)(2,1)S(1)} %get-tuple-element.8) | copy-start | bytes 12582916
  63.2 0.7 copy-start.1
